TPU v7x, 256 devices: a 4x2x16 block of a 4x16x16 slice. The times are simulated.
256 devices in a mesh: parts: 2 (over y), samp: 128 (over z, x, core).
Axes of the slice: x: 4, y: 2, z: 16, core: 2. Of those that a mesh axis runs over, the one named last changes fastest.
The devices are a block of a 4x16x16 slice.
Arguments:
- expression: bfloat16 [8192, 20480], P(('parts', 'samp')), parts along dimension 0, may hold values from -24 to 24
- current: bfloat16 [8192, 256], P(('parts', 'samp')), parts along dimension 0, may hold values from -6 to 6
- next_packed: int32 [512, 256], P(('parts', 'samp')), parts along dimension 0, may hold values from -2147483648 to 1789569706, as said below
- covariates: float32 [8192, 64], P(('parts', 'samp')), parts along dimension 0, may hold values from -1 to 1
Outputs:
- scores: float32 [40960, 256], P(('parts', 'samp')), parts along dimension 0
- next_block: bfloat16 [8192, 256], P(('parts', 'samp')), parts along dimension 0
There are 2 independent parts, one for each index of `parts`. A program takes and returns all parts, laid end to end along the dimension named above; each array names one. Nothing has to cross between parts.
Inputs may be any that keep to these rules, and one draw needn't show every extreme that they name: Each word holds the dosages (0, 1 or 2) of 16 consecutive samples of one variant, two bits a sample: sample 16 w + j of variant v in bits 2 j and 2 j + 1 of next_packed[v, w], bit 31 being the sign bit of the int32 word.
All inputs are finite; a program needn't handle non-finite values.
Results may differ from a plain program's by a relative error of at most 0.0004.
Values may be sent and summed in bfloat16 or wider, within the bound.
No kernel may reach another device: no remote copies, remote signals or barrier semaphores. Data moves between devices by JAX's collectives and lax.ppermute only.
A program may use at most 64 MiB of HBM per device.

v0:
```python
import functools
import jax
import jax.numpy as jnp
from jax import lax
from jax.sharding import Mesh
from jax.sharding import PartitionSpec as P

SAMP = ("samp_0", "samp_1", "samp_2")
PARTS_SAMP = ("parts", "samp_0", "samp_1", "samp_2")


def one_axis_at_a_time(array, axes):
    return functools.reduce(lax.psum, axes, array)


def unpack_words(packed_words):
    shifts = 2 * jnp.arange(16, dtype=jnp.int32)
    fields = jnp.bitwise_and(
        lax.shift_right_logical(packed_words[:, :, None], shifts[None, None, :]), 3
    )
    return fields.reshape(packed_words.shape[0], -1).T.astype(jnp.float32)


def over_samples(left, right):
    return lax.dot_general(
        left, right, (((0,), (0,)), ((), ())), preferred_element_type=jnp.float32
    )


def precise_samples(left, right):
    return lax.dot_general(left, right, (((0,), (0,)), ((), ())), precision=lax.Precision.HIGHEST)


def shards(expression, current, next_packed, covariates):
    group_size = lax.axis_size(SAMP)
    samples_all = expression.shape[0] * group_size
    scale_factor = float(samples_all) ** (-0.5)
    regrouped = lax.all_to_all(expression, SAMP, split_axis=1, concat_axis=0, tiled=True)
    scores = (
        over_samples(regrouped, lax.all_gather(current, SAMP, axis=0, tiled=True)) * scale_factor
    )
    packed_words = lax.all_to_all(next_packed, SAMP, split_axis=1, concat_axis=0, tiled=True)
    dosage = unpack_words(packed_words)
    local_totals = jnp.sum(dosage, axis=0)
    local_proj = precise_samples(covariates, dosage)
    local_covsum = jnp.sum(covariates, axis=0)
    totals, projected, cov_sums = (
        one_axis_at_a_time(local_totals, SAMP),
        one_axis_at_a_time(local_proj, SAMP),
        one_axis_at_a_time(local_covsum, SAMP),
    )
    average = totals / samples_all
    loading = projected - cov_sums[:, None] * average[None, :]
    leftover = (
        dosage - average[None, :] - jnp.dot(covariates, loading, precision=lax.Precision.HIGHEST)
    )
    sq_norm = one_axis_at_a_time(jnp.sum(leftover * leftover, axis=0), SAMP)
    next_block = (leftover * lax.rsqrt(sq_norm / samples_all + 1e-05)[None, :]).astype(jnp.bfloat16)
    return (scores, next_block)


def solution(mesh):
    split = Mesh(
        mesh.devices.reshape(mesh.shape["parts"], 16, 4, 2), ("parts", "samp_0", "samp_1", "samp_2")
    )
    in_specs = (P(PARTS_SAMP, None), P(PARTS_SAMP, None), P(PARTS_SAMP, None), P(PARTS_SAMP, None))
    out_specs = (P(PARTS_SAMP, None), P(PARTS_SAMP, None))
    return jax.shard_map(
        shards, mesh=split, in_specs=in_specs, out_specs=out_specs, check_vma=False
    )
```

profile of v0, /device:TPU:33, one launch (start us, length us, event | category | flops | bytes accessed | tf_op | source)
XLA Modules:
  0.0 414.3 jit_solution(10181218120002922908)
XLA Ops:
  8.0 0.8 all_to_all.30
  8.9 0.8 copy.9
  9.6 31.0 %all-to-all-start.1 = ((s32[2,128,2]{2,0,1:T(2,128)}), s32[2,128,2]{2,0,1:T(2,128)S(1)}, u32[]{:S(2)}, u32[]{:S(2)}) async-start(s32[2,128,2]{2,0,1:T(2,128)} %copy.9), calls=%async_computation.1 | async-start | bytes 262144 | tf_op jit(solution)/shard_map/all_to_all | solution.py:42
  40.6 3.6 all_to_all.26
  44.3 2.5 copy.8
  46.8 0.0 copy-start
  46.8 9.7 %all-to-all-done.1 = s32[2,128,2]{2,0,1:T(2,128)S(1)} async-done(((s32[2,128,2]{2,0,1:T(2,128)}), s32[2,128,2]{2,0,1:T(2,128)S(1)}, u32[]{:S(2)}, u32[]{:S(2)}) %all-to-all-start.1) | async-done | bytes 2080 | tf_op jit(solution)/shard_map/all_to_all | solution.py:42
  56.5 9.1 %all-to-all-start = ((bf16[32,128,160]{2,0,1:T(8,128)(2,1)}), bf16[32,128,160]{2,0,1:T(8,128)(2,1)S(1)}, u32[]{:S(2)}, u32[]{:S(2)}) async-start(bf16[32,128,160]{2,0,1:T(8,128)(2,1)} %copy.8), calls=%async_computation | async-start | bytes 4194304 | tf_op jit(solution)/shard_map/all_to_all | solution.py:38
  65.5 0.1 all-reduce.7.cloned.1.call-start
  65.6 0.1 shift_right_logical.26
  65.7 0.1 copy.11
  65.8 0.1 fusion.3
  65.9 0.0 copy-done
  65.9 0.9 convolution_bitcast_fusion
  66.8 0.1 all-reduce.7.cloned.1.call-update
  66.8 0.1 all-reduce.9.cloned.1.call-start
  66.9 132.8 %all-reduce.7.cloned.1.call-done = f32[64,256]{1,0:T(8,128)} async-done(((f32[64,256]{1,0:T(8,128)}), f32[64,256]{1,0:T(8,128)}) %all-reduce.7.cloned.1.call-update) | async-done | bytes 65552 | tf_op jit(solution)/shard_map/psum | solution.py:13
  199.7 0.1 all-reduce.9.cloned.1.call-update
  199.8 0.1 all-reduce.11.cloned.1.call-start
  199.8 60.7 %all-reduce.9.cloned.1.call-done = f32[64,256]{1,0:T(8,128)} async-done(((f32[64,256]{1,0:T(8,128)}), f32[64,256]{1,0:T(8,128)}) %all-reduce.9.cloned.1.call-update) | async-done | bytes 65552 | tf_op jit(solution)/shard_map/psum | solution.py:13
  260.6 0.1 all-reduce.11.cloned.1.call-update
  260.6 0.1 all-gather.2.cloned.1.call-start
  260.7 0.6 all-gather.2.cloned.1.call-update
  261.3 0.1 fusion.6
  261.4 24.5 %all-reduce = (f32[256]{0:T(256)S(1)}, f32[64]{0:T(128)S(1)}) all-reduce(f32[256]{0:T(256)S(1)} %fusion.6, f32[64]{0:T(128)S(1)} %reduce_sum.28), channel_id=1, replica_groups=mesh['parts'=2,'samp_0'=16,'samp_1'=4,'samp_2'=2] {'samp_0'}, use_global_device_ids=true, to_apply=%region_1.0 | all-reduce | flops 320 | bytes 2560 | tf_op jit(solution)/shard_map/psum | solution.py:13
  285.9 7.2 %all-reduce.1 = (f32[256]{0:T(256)S(1)}, f32[64]{0:T(128)S(1)}) all-reduce(f32[256]{0:T(256)S(1)} %get-tuple-element.2, f32[64]{0:T(128)S(1)} %get-tuple-element.3), channel_id=1, replica_groups=mesh['parts'=2,'samp_0'=16,'samp_1'=4,'samp_2'=2] {'samp_1'}, use_global_device_ids=true, to_apply=%region_2.0 | all-reduce | flops 320 | bytes 2560 | tf_op jit(solution)/shard_map/psum | solution.py:13
  293.1 13.6 %all-reduce.2 = (f32[256]{0:T(256)S(1)}, f32[64]{0:T(128)S(1)}) all-reduce(f32[256]{0:T(256)S(1)} %get-tuple-element.4, f32[64]{0:T(128)S(1)} %get-tuple-element.5), channel_id=1, replica_groups=mesh['parts'=2,'samp_0'=16,'samp_1'=4,'samp_2'=2] {'samp_2'}, use_global_device_ids=true, to_apply=%region_3.0 | all-reduce | flops 320 | bytes 2560 | tf_op jit(solution)/shard_map/psum | solution.py:13
  306.6 0.0 all-reduce.11.cloned.1.call-done
  306.6 1.1 multiply_reduce_fusion
  307.7 22.7 %psum.93 = f32[256]{0:T(256)S(1)} all-reduce(f32[256]{0:T(256)S(1)} %get-tuple-element.8), channel_id=1, replica_groups=mesh['parts'=2,'samp_0'=16,'samp_1'=4,'samp_2'=2] {'samp_0'}, use_global_device_ids=true, to_apply=%region_12.0 | all-reduce | flops 256 | bytes 2048 | tf_op jit(solution)/shard_map/psum | solution.py:13
  330.4 6.8 %psum.94 = f32[256]{0:T(256)S(1)} all-reduce(f32[256]{0:T(256)S(1)} %psum.93), channel_id=1, replica_groups=mesh['parts'=2,'samp_0'=16,'samp_1'=4,'samp_2'=2] {'samp_1'}, use_global_device_ids=true, to_apply=%region_13.0 | all-reduce | flops 256 | bytes 2048 | tf_op jit(solution)/shard_map/psum | solution.py:13
  337.3 9.7 %psum.95 = f32[256]{0:T(256)S(1)} all-reduce(f32[256]{0:T(256)S(1)} %psum.94), channel_id=1, replica_groups=mesh['parts'=2,'samp_0'=16,'samp_1'=4,'samp_2'=2] {'samp_2'}, use_global_device_ids=true, to_apply=%region_14.0 | all-reduce | flops 256 | bytes 2048 | tf_op jit(solution)/shard_map/psum | solution.py:13
  347.0 0.6 fusion.7
  347.6 56.6 %all-gather.2.cloned.1.call-done = bf16[4096,256]{1,0:T(8,128)(2,1)} async-done(((bf16[32,256]{1,0:T(8,128)(2,1)}), bf16[4096,256]{1,0:T(8,128)(2,1)}) %all-gather.2.cloned.1.call-update) | async-done | bytes 2097168 | tf_op jit(solution)/shard_map/all_gather | solution.py:40
  404.2 0.0 all-to-all-done
  404.2 3.0 convolution_multiply_fusion
  (5 shorter events, 0.0 us)
Async XLA Ops:
  9.6 46.8 %all-to-all-start.1 = ((s32[2,128,2]{2,0,1:T(2,128)}), s32[2,128,2]{2,0,1:T(2,128)S(1)}, u32[]{:S(2)}, u32[]{:S(2)}) async-start(s32[2,128,2]{2,0,1:T(2,128)} %copy.9), calls=%async_computation.1 | async-start | bytes 262144 | tf_op jit(solution)/shard_map/all_to_all | solution.py:42
  46.8 19.1 %copy-start = (f32[32,64]{1,0:T(8,128)S(1)}, f32[32,64]{1,0:T(8,128)}, u32[]{:S(2)}) copy-start(f32[32,64]{1,0:T(8,128)} %param.7) | copy-start | bytes 24580
  56.5 347.7 %all-to-all-start = ((bf16[32,128,160]{2,0,1:T(8,128)(2,1)}), bf16[32,128,160]{2,0,1:T(8,128)(2,1)S(1)}, u32[]{:S(2)}, u32[]{:S(2)}) async-start(bf16[32,128,160]{2,0,1:T(8,128)(2,1)} %copy.8), calls=%async_computation | async-start | bytes 4194304 | tf_op jit(solution)/shard_map/all_to_all | solution.py:38
  65.5 134.2 %all-reduce.7.cloned.1.call-start = ((), (), s32[]{:S(2)}) async-start(), calls=%async_computation.3 | async-start | bytes 131072 | tf_op jit(solution)/shard_map/psum | solution.py:13
  66.8 193.7 %all-reduce.9.cloned.1.call-start = ((), (), s32[]{:S(2)}) async-start(), calls=%async_computation.4 | async-start | bytes 131072 | tf_op jit(solution)/shard_map/psum | solution.py:13
  199.8 106.9 %all-reduce.11.cloned.1.call-start = ((), (), s32[]{:S(2)}) async-start(), calls=%async_computation.5 | async-start | bytes 131072 | tf_op jit(solution)/shard_map/psum | solution.py:13
  260.6 143.6 %all-gather.2.cloned.1.call-start = ((), (), s32[]{:S(2)}) async-start(), calls=%async_computation.2 | async-start | bytes 2113536 | tf_op jit(solution)/shard_map/all_gather | solution.py:40
Sparse Core Ops, SparseCore 0:
  69.3 130.3 all-reduce.6
  202.0 58.4 all-reduce.8
  263.1 39.1 all-reduce.10
Sparse Core Ops, SparseCore 1:
  263.7 140.4 all-gather.1
where the time goes:
time: 415 us; the launch traced here: 414 us
  waiting for transfers between devices  261 us (63%)
  blocking collectives  84.5 us (20%)
  starting transfers between devices  40.3 us (10%)
  between operations  15.3 us (4%)
  local copies, waits for them, and re-layouts  7.9 us (2%)
  matrix products  4.96 us (1%)
    psum x3, waiting for transfers between devices, one_axis_at_a_time(): return functools.reduce(lax.psum, axes, array)  194 us
    psum x6, blocking collectives, one_axis_at_a_time(): return functools.reduce(lax.psum, axes, array)  84.5 us
    all_gather x1, waiting for transfers between devices, shards(): lax.all_gather(current, SAMP, axis=0, tiled=True)  56.6 us
    all_to_all x1, starting transfers between devices, shards(): lax.all_to_all(next_packed, SAMP, split_axis=1, concat_axis=0, tiled=True)  31 us
    all_to_all x1, waiting for transfers between devices, shards(): lax.all_to_all(next_packed, SAMP, split_axis=1, concat_axis=0, tiled=True)  9.66 us
    all_to_all x1, starting transfers between devices, shards(): lax.all_to_all(expression, SAMP, split_axis=1, concat_axis=0, tiled=True)  9.06 us
  transfers between devices with their start and end apart: 6, of which 4 were waited for; matrix products, arithmetic and copies ran while one was open for 1% of the time, Pallas kernels for 0%

commit v1 on v0

--- a/solution.py
+++ b/solution.py
@@ -7,6 +7,11 @@
 
 SAMP = ("samp_0", "samp_1", "samp_2")
 PARTS_SAMP = ("parts", "samp_0", "samp_1", "samp_2")
+
+
+def all_by_exchange(block, name, d):
+    sent = jnp.stack([block] * lax.axis_size(name))
+    return jnp.concatenate(lax.all_to_all(sent, name, 0, 0), axis=d)
 
 
 def one_axis_at_a_time(array, axes):
@@ -36,9 +41,7 @@
     samples_all = expression.shape[0] * group_size
     scale_factor = float(samples_all) ** (-0.5)
     regrouped = lax.all_to_all(expression, SAMP, split_axis=1, concat_axis=0, tiled=True)
-    scores = (
-        over_samples(regrouped, lax.all_gather(current, SAMP, axis=0, tiled=True)) * scale_factor
-    )
+    scores = over_samples(regrouped, all_by_exchange(current, SAMP, 0)) * scale_factor
     packed_words = lax.all_to_all(next_packed, SAMP, split_axis=1, concat_axis=0, tiled=True)
     dosage = unpack_words(packed_words)
     local_totals = jnp.sum(dosage, axis=0)

time: 415 us -> 470 us (1.13)
  blocking collectives: 84.5 us -> 200 us
  waiting for transfers between devices: 261 us -> 193 us
    all_to_all x0 -> x1, blocking collectives: none -> 105 us  [shards(): lax.all_to_all(expression, SAMP, split_axis=1, concat_axis=0, tiled=True)]
    all_gather x1 -> x0, waiting for transfers between devices: 56.6 us -> none  [shards(): lax.all_gather(current, SAMP, axis=0, tiled=True)]
    psum x6, blocking collectives: 84.5 us -> 95.4 us  [one_axis_at_a_time(): return functools.reduce(lax.psum, axes, array)]
    psum x3, waiting for transfers between devices: 194 us -> 183 us  [one_axis_at_a_time(): return functools.reduce(lax.psum, axes, array)]
  transfers between devices with their start and end apart: 6 -> 5, of which waited for: 4 -> 4; matrix products, arithmetic and copies ran while one was open for 1% -> 2% of each run, Pallas kernels for 0% -> 0%
where the time goes in v1:
time: 470 us; the launch traced here: 469 us
  blocking collectives  200 us (43%)
  waiting for transfers between devices  193 us (41%)
  starting transfers between devices  43.6 us (9%)
  between operations  13.9 us (3%)
  local copies, waits for them, and re-layouts  11.5 us (2%)
  matrix products  6.64 us (1%)
    psum x3, waiting for transfers between devices, one_axis_at_a_time(): return functools.reduce(lax.psum, axes, array)  183 us
    all_to_all x1, blocking collectives, shards(): lax.all_to_all(expression, SAMP, split_axis=1, concat_axis=0, tiled=True)  105 us
    psum x6, blocking collectives, one_axis_at_a_time(): return functools.reduce(lax.psum, axes, array)  95.4 us
    all_to_all x1, starting transfers between devices, shards(): lax.all_to_all(next_packed, SAMP, split_axis=1, concat_axis=0, tiled=True)  31 us
    all_to_all x1, starting transfers between devices, all_by_exchange(): return jnp.concatenate(lax.all_to_all(sent, name, 0, 0), axis=d)  12.4 us
    all_to_all x1, waiting for transfers between devices, shards(): lax.all_to_all(next_packed, SAMP, split_axis=1, concat_axis=0, tiled=True)  9.65 us
  transfers between devices with their start and end apart: 5, of which 4 were waited for; matrix products, arithmetic and copies ran while one was open for 2% of the time, Pallas kernels for 0%

profile of v1, /device:TPU:33, one launch (start us, length us, event | category | flops | bytes accessed | tf_op | source)
XLA Modules:
  0.0 469.2 jit_solution(4419667494863788325)
XLA Ops:
  7.2 0.8 all_to_all.31
  8.0 0.8 copy.11
  8.8 31.0 %all-to-all-start.2 = ((s32[2,128,2]{2,0,1:T(2,128)}), s32[2,128,2]{2,0,1:T(2,128)S(1)}, u32[]{:S(2)}, u32[]{:S(2)}) async-start(s32[2,128,2]{2,0,1:T(2,128)} %copy.11), calls=%async_computation.2 | async-start | bytes 262144 | tf_op jit(solution)/shard_map/all_to_all | solution.py:45
  39.8 3.6 all_to_all.27
  43.4 2.5 copy.8
  46.0 0.0 copy-start.1
  46.0 9.6 %all-to-all-done.2 = s32[2,128,2]{2,0,1:T(2,128)S(1)} async-done(((s32[2,128,2]{2,0,1:T(2,128)}), s32[2,128,2]{2,0,1:T(2,128)S(1)}, u32[]{:S(2)}, u32[]{:S(2)}) %all-to-all-start.2) | async-done | bytes 2080 | tf_op jit(solution)/shard_map/all_to_all | solution.py:45
  55.6 104.6 %all_to_all.37 = bf16[32,128,160]{2,0,1:T(8,128)(2,1)S(1)} all-to-all(bf16[32,128,160]{2,0,1:T(8,128)(2,1)} %copy.8), channel_id=1, replica_groups=mesh['parts'=2,'samp_0'=16,'samp_1'=4,'samp_2'=2] {'samp_0','samp_1','sa..., dimensions={1} | all-to-all | bytes 2621440 | tf_op jit(solution)/shard_map/all_to_all | solution.py:43
  160.2 0.0 copy-done.1
  160.2 1.6 stack.2
  161.7 0.0 copy-start
  161.7 12.4 %all-to-all-start.1 = ((bf16[128,32,256]{2,1,0:T(8,128)(2,1)}), bf16[128,32,256]{2,1,0:T(8,128)(2,1)}, u32[]{:S(2)}, u32[]{:S(2)}) async-start(bf16[128,32,256]{2,1,0:T(8,128)(2,1)} %stack.2), calls=%async_computation.1 | async-start | bytes 4194304 | tf_op jit(solution)/shard_map/all_to_all | solution.py:14
  174.1 0.1 all-reduce.7.cloned.1.call-start
  174.2 0.1 shift_right_logical.26
  174.3 0.1 copy.13
  174.4 0.1 fusion.16
  174.5 0.0 copy-done
  174.5 0.9 convolution_bitcast_fusion
  175.4 0.1 all-reduce.7.cloned.1.call-update
  175.4 0.1 all-reduce.9.cloned.1.call-start
  175.5 132.9 %all-reduce.7.cloned.1.call-done = f32[64,256]{1,0:T(8,128)} async-done(((f32[64,256]{1,0:T(8,128)}), f32[64,256]{1,0:T(8,128)}) %all-reduce.7.cloned.1.call-update) | async-done | bytes 65552 | tf_op jit(solution)/shard_map/psum | solution.py:18
  308.3 0.1 all-reduce.9.cloned.1.call-update
  308.4 0.1 all-reduce.11.cloned.1.call-start
  308.5 0.1 fusion.19
  308.6 21.6 %all-reduce = (f32[256]{0:T(256)S(1)}, f32[64]{0:T(128)S(1)}) all-reduce(f32[256]{0:T(256)S(1)} %fusion.19, f32[64]{0:T(128)S(1)} %reduce_sum.28), channel_id=1, replica_groups=mesh['parts'=2,'samp_0'=16,'samp_1'=4,'samp_2'=2] {'samp_0'}, use_global_device_ids=true, to_apply=%region_1.0 | all-reduce | flops 320 | bytes 2560 | tf_op jit(solution)/shard_map/psum | solution.py:18
  330.2 8.8 %all-reduce.1 = (f32[256]{0:T(256)S(1)}, f32[64]{0:T(128)S(1)}) all-reduce(f32[256]{0:T(256)S(1)} %get-tuple-element.2, f32[64]{0:T(128)S(1)} %get-tuple-element.3), channel_id=1, replica_groups=mesh['parts'=2,'samp_0'=16,'samp_1'=4,'samp_2'=2] {'samp_1'}, use_global_device_ids=true, to_apply=%region_2.0 | all-reduce | flops 320 | bytes 2560 | tf_op jit(solution)/shard_map/psum | solution.py:18
  339.0 21.7 %all-reduce.2 = (f32[256]{0:T(256)S(1)}, f32[64]{0:T(128)S(1)}) all-reduce(f32[256]{0:T(256)S(1)} %get-tuple-element.4, f32[64]{0:T(128)S(1)} %get-tuple-element.5), channel_id=1, replica_groups=mesh['parts'=2,'samp_0'=16,'samp_1'=4,'samp_2'=2] {'samp_2'}, use_global_device_ids=true, to_apply=%region_3.0 | all-reduce | flops 320 | bytes 2560 | tf_op jit(solution)/shard_map/psum | solution.py:18
  360.7 8.5 %all-reduce.9.cloned.1.call-done = f32[64,256]{1,0:T(8,128)} async-done(((f32[64,256]{1,0:T(8,128)}), f32[64,256]{1,0:T(8,128)}) %all-reduce.9.cloned.1.call-update) | async-done | bytes 65552 | tf_op jit(solution)/shard_map/psum | solution.py:18
  369.2 0.1 all-reduce.11.cloned.1.call-update
  369.3 41.7 %all-reduce.11.cloned.1.call-done = f32[64,256]{1,0:T(8,128)} async-done(((f32[64,256]{1,0:T(8,128)}), f32[64,256]{1,0:T(8,128)}) %all-reduce.11.cloned.1.call-update) | async-done | bytes 65552 | tf_op jit(solution)/shard_map/psum | solution.py:18
  411.0 1.1 multiply_reduce_fusion
  412.1 23.9 %psum.93 = f32[256]{0:T(256)S(1)} all-reduce(f32[256]{0:T(256)S(1)} %get-tuple-element.8), channel_id=1, replica_groups=mesh['parts'=2,'samp_0'=16,'samp_1'=4,'samp_2'=2] {'samp_0'}, use_global_device_ids=true, to_apply=%region_12.0 | all-reduce | flops 256 | bytes 2048 | tf_op jit(solution)/shard_map/psum | solution.py:18
  436.0 8.4 %psum.94 = f32[256]{0:T(256)S(1)} all-reduce(f32[256]{0:T(256)S(1)} %psum.93), channel_id=1, replica_groups=mesh['parts'=2,'samp_0'=16,'samp_1'=4,'samp_2'=2] {'samp_1'}, use_global_device_ids=true, to_apply=%region_13.0 | all-reduce | flops 256 | bytes 2048 | tf_op jit(solution)/shard_map/psum | solution.py:18
  444.4 11.0 %psum.95 = f32[256]{0:T(256)S(1)} all-reduce(f32[256]{0:T(256)S(1)} %psum.94), channel_id=1, replica_groups=mesh['parts'=2,'samp_0'=16,'samp_1'=4,'samp_2'=2] {'samp_2'}, use_global_device_ids=true, to_apply=%region_14.0 | all-reduce | flops 256 | bytes 2048 | tf_op jit(solution)/shard_map/psum | solution.py:18
  455.4 0.6 fusion.20
  456.0 2.0 copy.9
  458.0 0.0 all-to-all-done.1
  458.0 4.6 fusion.8
  (5 shorter events, 0.0 us)
Async XLA Ops:
  8.8 46.8 %all-to-all-start.2 = ((s32[2,128,2]{2,0,1:T(2,128)}), s32[2,128,2]{2,0,1:T(2,128)S(1)}, u32[]{:S(2)}, u32[]{:S(2)}) async-start(s32[2,128,2]{2,0,1:T(2,128)} %copy.11), calls=%async_computation.2 | async-start | bytes 262144 | tf_op jit(solution)/shard_map/all_to_all | solution.py:45
  46.0 114.2 %copy-start.1 = (bf16[32,256]{1,0:T(8,128)(2,1)S(1)}, bf16[32,256]{1,0:T(8,128)(2,1)}, u32[]{:S(2)}) copy-start(bf16[32,256]{1,0:T(8,128)(2,1)} %param.5) | copy-start | bytes 49156
  161.7 12.7 %copy-start = (f32[32,64]{1,0:T(8,128)S(1)}, f32[32,64]{1,0:T(8,128)}, u32[]{:S(2)}) copy-start(f32[32,64]{1,0:T(8,128)} %param.7) | copy-start | bytes 24580
  161.7 296.3 %all-to-all-start.1 = ((bf16[128,32,256]{2,1,0:T(8,128)(2,1)}), bf16[128,32,256]{2,1,0:T(8,128)(2,1)}, u32[]{:S(2)}, u32[]{:S(2)}) async-start(bf16[128,32,256]{2,1,0:T(8,128)(2,1)} %stack.2), calls=%async_computation.1 | async-start | bytes 4194304 | tf_op jit(solution)/shard_map/all_to_all | solution.py:14
  174.1 134.2 %all-reduce.7.cloned.1.call-start = ((), (), s32[]{:S(2)}) async-start(), calls=%async_computation.3 | async-start | bytes 131072 | tf_op jit(solution)/shard_map/psum | solution.py:18
  175.4 193.8 %all-reduce.9.cloned.1.call-start = ((), (), s32[]{:S(2)}) async-start(), calls=%async_computation.4 | async-start | bytes 131072 | tf_op jit(solution)/shard_map/psum | solution.py:18
  308.4 102.6 %all-reduce.11.cloned.1.call-start = ((), (), s32[]{:S(2)}) async-start(), calls=%async_computation.5 | async-start | bytes 131072 | tf_op jit(solution)/shard_map/psum | solution.py:18
Sparse Core Ops, SparseCore 0:
  177.9 130.4 all-reduce.6
  310.7 58.4 all-reduce.8
  371.8 39.1 all-reduce.10
